TPU v7x, 128 devices: a whole 4x4x4 slice. The times are simulated.
128 devices in a mesh: data: 1, stage: 128 (over z, y, x, core).
Axes of the slice: x: 4, y: 4, z: 4, core: 2. Of those that a mesh axis runs over, the one named last changes fastest.
Arguments:
- x_enc: bfloat16 [128, 1024, 1024], P(('data', 'stage'))
- enc_len: int32 [128], P(('data', 'stage'))
- y: bfloat16 [128, 64, 1024], P(('data', 'stage'))
- enc_wqkv: bfloat16 [2, 1024, 3, 16, 128], replicated
- enc_wo: bfloat16 [2, 16, 128, 1024], replicated
- enc_w1: bfloat16 [2, 1024, 3072], replicated
- enc_w2: bfloat16 [2, 3072, 1024], replicated
- dec_wqkv: bfloat16 [2, 1024, 3, 16, 128], replicated
- dec_wo: bfloat16 [2, 16, 128, 1024], replicated
- cross_wq: bfloat16 [2, 1024, 8, 2, 128], replicated
- cross_wkv: bfloat16 [2, 1024, 2, 8, 128], replicated
- cross_wo: bfloat16 [2, 8, 2, 128, 1024], replicated
- dec_w1: bfloat16 [2, 1024, 3072], replicated
- dec_w2: bfloat16 [2, 3072, 1024], replicated
Outputs:
- output: bfloat16 [128, 64, 1024], P(('data', 'stage'))
All inputs are finite; a program needn't handle non-finite values.
Results may differ from a plain program's by a relative error of at most 0.0129945.
Values are sent between devices in bfloat16 or wider.
A program may use at most 1 GiB of HBM per device.

v0:
```python
import jax
import jax.numpy as jnp
from jax import lax
from jax.sharding import PartitionSpec as P, NamedSharding


def rms_norm(inputs):
    wide = inputs.astype(jnp.float32)
    return (wide * lax.rsqrt(jnp.mean(wide * wide, axis=-1, keepdims=True) + 1e-6)).astype(jnp.bfloat16)


def attend(query, keys, values, valid):
    scale = query.shape[-1] ** -0.5
    scores = jnp.einsum("bqgrd,bkgd->bgrqk", query, keys, preferred_element_type=jnp.float32) * scale
    attn_probs = jax.nn.softmax(jnp.where(valid, scores, -1e30), axis=-1).astype(jnp.bfloat16)
    return jnp.einsum("bgrqk,bkgd->bqgrd", attn_probs, values, preferred_element_type=jnp.float32).astype(jnp.bfloat16)


def self_block(state, w_qkv, w_out, valid):
    proj_qkv = jnp.einsum("bsd,dthe->tbshe", rms_norm(state), w_qkv, preferred_element_type=jnp.float32).astype(jnp.bfloat16)
    mixed = attend(proj_qkv[0][:, :, :, None, :], proj_qkv[1], proj_qkv[2], valid)
    update = jnp.einsum("bshre,hev->bsv", mixed, w_out, preferred_element_type=jnp.float32)
    return (state.astype(jnp.float32) + update).astype(jnp.bfloat16)


def ffn_block(state, w_in, w_out):
    hidden = jax.nn.gelu(jnp.einsum("bsd,df->bsf", rms_norm(state), w_in, preferred_element_type=jnp.float32)).astype(jnp.bfloat16)
    update = jnp.einsum("bsf,fd->bsd", hidden, w_out, preferred_element_type=jnp.float32)
    return (state.astype(jnp.float32) + update).astype(jnp.bfloat16)


def encoder(x_enc, enc_len, enc_wqkv, enc_wo, enc_w1, enc_w2):
    valid = (jnp.arange(x_enc.shape[1])[None, :] < enc_len[:, None])[:, None, None, None, :]
    state = x_enc
    for layer in range(enc_wqkv.shape[0]):
        state = self_block(state, enc_wqkv[layer], enc_wo[layer], valid)
        state = ffn_block(state, enc_w1[layer], enc_w2[layer])
    return rms_norm(state)


def decoder(y, kv_all, kv_len, dec_wqkv, dec_wo, cross_wq, cross_wo, dec_w1, dec_w2):
    positions = jnp.arange(y.shape[1])
    causal = positions[None, :] <= positions[:, None]
    keep = (jnp.arange(kv_all.shape[3])[None, :] < kv_len[:, None])[:, None, None, None, :]
    state = y
    for layer in range(dec_wqkv.shape[0]):
        state = self_block(state, dec_wqkv[layer], dec_wo[layer], causal)
        query = jnp.einsum("bsd,dgre->bsgre", rms_norm(state), cross_wq[layer], preferred_element_type=jnp.float32).astype(jnp.bfloat16)
        mixed = attend(query, kv_all[layer, 0], kv_all[layer, 1], keep)
        update = jnp.einsum("bsgre,grev->bsv", mixed, cross_wo[layer], preferred_element_type=jnp.float32)
        state = (state.astype(jnp.float32) + update).astype(jnp.bfloat16)
        state = ffn_block(state, dec_w1[layer], dec_w2[layer])
    return state


def solution(mesh):
    stages = mesh.shape["stage"]
    swap = [(source, (source + stages // 2) % stages) for source in range(stages)]
    rows = P(("data", "stage"))
    whole = P()

    def body(x_enc, enc_len, y, enc_wqkv, enc_wo, enc_w1, enc_w2, dec_wqkv, dec_wo, cross_wq, cross_wkv, cross_wo, dec_w1, dec_w2):
        enc_out = encoder(x_enc, enc_len, enc_wqkv, enc_wo, enc_w1, enc_w2)
        kv_all = jnp.einsum("bsd,ldtge->ltbsge", enc_out, cross_wkv, preferred_element_type=jnp.float32).astype(jnp.bfloat16)
        kv_recv = lax.ppermute(kv_all, "stage", swap)
        len_recv = lax.ppermute(enc_len, "stage", swap)
        return decoder(y, kv_recv, len_recv, dec_wqkv, dec_wo, cross_wq, cross_wo, dec_w1, dec_w2)

    return jax.shard_map(body, mesh=mesh, in_specs=(rows, rows, rows) + (whole,) * 11, out_specs=rows, check_vma=False)
```

profile of v0, /device:TPU:0, one launch (start us, length us, event | category | flops | bytes accessed | tf_op | source)
XLA Modules:
  0.0 544.2 jit_solution(6292897297587748712)
XLA Ops:
  0.0 2.9 copy.17
  2.9 0.0 copy-start
  2.9 0.5 fusion.70
  3.4 18.8 %fusion.391 = (bf16[1,1024,3,16,128]{4,3,2,1,0:T(8,128)(2,1)}, bf16[1,1024,3,16,128]{4,3,2,1,0:T(8,128)(2,1)}) fusion(bf16[2,1024,3,16,128]{4,3,2,1,0:T(8,128)(2,1)} %param.17), kind=kLoop, calls=%fused_computation.325 | loop fusion | bytes 50331648 | tf_op jit(solution)/shard_map/slice | solution.py:36
  22.8 0.0 copy-done
  22.8 22.7 %convert_bitcast_fusion.1 = bf16[3,1,1024,16,128]{4,2,3,0,1:T(8,128)(2,1)} fusion(bf16[1,1024,3,16,128]{4,3,2,1,0:T(8,128)(2,1)} %get-tuple-element.8, bf16[1,1024,1024]{1,2,0:T(8,128)(2,1)S(1)} %copy.17, f32[1024]{0:T(1024)S(1)} %add_rsqrt_fusion.4), kind=kOutput, calls=%fused_computation.43 | convolution fusion | flops 12894339072 | bytes 27267072 | tf_op jit(solution)/shard_map/bsd,dthe->tbshe/dot_general | solution.py:20
  45.5 27.4 %bitcast_reduce_fusion.1 = (f32[16,1024]{1,0:T(8,128)S(1)}, f32[16,1024,1024]{2,1,0:T(8,128)}) fusion(pred[1024]{0:T(1024)(128)(4,1)S(1)} %iota_compare_fusion.2, bf16[3,1,1024,16,128]{4,2,3,0,1:T(8,128)(2,1)} %convert_bitcast_fusion.1), kind=kOutput, calls=%fused_computation.5 | convolution fusion | flops 4345282560 | bytes 75564032 | tf_op jit(solution)/shard_map/bqgrd,bkgd->bgrqk/dot_general | solution.py:14
  72.9 21.4 %fusion.2 = f32[16,1024]{1,0:T(8,128)S(1)} fusion(f32[16,1024,1024]{2,1,0:T(8,128)} %get-tuple-element.14, f32[16,1024]{1,0:T(8,128)S(1)} %get-tuple-element.13, pred[1024]{0:T(1024)(128)(4,1)S(1)} %iota_compare_fusion.2), kind=kLoop, calls=%fused_computation.10 | loop fusion | flops 67092480 | bytes 67240960 | tf_op jit(solution)/shard_map/reduce_sum | solution.py:15
  94.4 0.0 copy-start.1
  94.4 29.6 %fusion.171.clone.5 = bf16[1024,16,128]{0,2,1:T(8,128)(2,1)} fusion(f32[16,1024]{1,0:T(8,128)S(1)} %fusion.2, f32[16,1024]{1,0:T(8,128)S(1)} %get-tuple-element.13, f32[16,1024,1024]{2,1,0:T(8,128)} %get-tuple-element.14, pred[1024]{0:T(1024)(128)(4,1)S(1)} %iota_compare_fusion.2, ...), kind=kOutput, calls=%fused_computation.118.clone.clone.clone.clone.clone.2 | convolution fusion | flops 4380950528 | bytes 75629568 | tf_op jit(solution)/shard_map/bgrqk,bkgd->bqgrd/dot_general | solution.py:16
  123.9 0.0 copy-done.1
  123.9 9.8 %fusion.73 = (f32[1024]{0:T(1024)S(1)}, bf16[1,1024,1024]{1,2,0:T(8,128)(2,1)}) fusion(bf16[2,16,128,1024]{3,2,1,0:T(8,128)(2,1)} %param.18, bf16[1,1024,1024]{1,2,0:T(8,128)(2,1)S(1)} %copy-done.1, bf16[1024,16,128]{0,2,1:T(8,128)(2,1)} %fusion.171.clone.5), kind=kOutput, calls=%fused_computation.96 | convolution fusion | flops 4301257728 | bytes 12587008 | tf_op jit(solution)/shard_map/bshre,hev->bsv/dot_general | solution.py:22
  133.7 20.8 %fusion.76 = (f32[1024]{0:T(1024)S(1)}, bf16[1,1024,1024]{1,2,0:T(8,128)(2,1)S(1)}) fusion(bf16[2,3072,1024]{2,1,0:T(8,128)(2,1)} %param.20, bf16[2,1024,3072]{2,1,0:T(8,128)(2,1)} %param.19, bf16[1,1024,1024]{1,2,0:T(8,128)(2,1)} %get-tuple-element.16, f32[1024]{0:T(1024)S(1)} %add_rsqrt_fusion.3), kind=kOutput, calls=%fused_computation.99 | convolution fusion | flops 12922649600 | bytes 18882560 | tf_op jit(solution)/shard_map/bsf,fd->bsd/dot_general | solution.py:28
  154.5 0.0 copy-start.3
  154.5 1.3 copy-done.3
  155.9 22.7 %convert_bitcast_fusion = bf16[3,1,1024,16,128]{4,2,3,0,1:T(8,128)(2,1)} fusion(bf16[1,1024,3,16,128]{4,3,2,1,0:T(8,128)(2,1)} %get-tuple-element.7, bf16[1,1024,1024]{1,2,0:T(8,128)(2,1)S(1)} %get-tuple-element.18, f32[1024]{0:T(1024)S(1)} %add_rsqrt_fusion.2), kind=kOutput, calls=%fused_computation.42 | convolution fusion | flops 12894339072 | bytes 27267072 | tf_op jit(solution)/shard_map/bsd,dthe->tbshe/dot_general | solution.py:20
  178.6 27.6 %bitcast_reduce_fusion = (f32[16,1024]{1,0:T(8,128)S(1)}, f32[16,1024,1024]{2,1,0:T(8,128)}) fusion(pred[1024]{0:T(1024)(128)(4,1)S(1)} %iota_compare_fusion.2, bf16[3,1,1024,16,128]{4,2,3,0,1:T(8,128)(2,1)} %convert_bitcast_fusion), kind=kOutput, calls=%fused_computation.1 | convolution fusion | flops 4345282560 | bytes 75564032 | tf_op jit(solution)/shard_map/bqgrd,bkgd->bgrqk/dot_general | solution.py:14
  206.2 21.4 %fusion.3 = f32[16,1024]{1,0:T(8,128)S(1)} fusion(f32[16,1024,1024]{2,1,0:T(8,128)} %get-tuple-element.20, f32[16,1024]{1,0:T(8,128)S(1)} %get-tuple-element.19, pred[1024]{0:T(1024)(128)(4,1)S(1)} %iota_compare_fusion.2), kind=kLoop, calls=%fused_computation.11 | loop fusion | flops 67092480 | bytes 67240960 | tf_op jit(solution)/shard_map/reduce_sum | solution.py:15
  227.6 29.4 %fusion.177.clone.5 = bf16[1024,16,128]{0,2,1:T(8,128)(2,1)} fusion(f32[16,1024]{1,0:T(8,128)S(1)} %fusion.3, f32[16,1024]{1,0:T(8,128)S(1)} %get-tuple-element.19, f32[16,1024,1024]{2,1,0:T(8,128)} %get-tuple-element.20, pred[1024]{0:T(1024)(128)(4,1)S(1)} %iota_compare_fusion.2, ...), kind=kOutput, calls=%fused_computation.117.clone.clone.clone.clone.clone.2 | convolution fusion | flops 4380950528 | bytes 75629568 | tf_op jit(solution)/shard_map/bgrqk,bkgd->bqgrd/dot_general | solution.py:16
  257.0 9.0 %fusion.79 = (f32[1024]{0:T(1024)S(1)}, bf16[1,1024,1024]{1,2,0:T(8,128)(2,1)S(1)}) fusion(bf16[2,16,128,1024]{3,2,1,0:T(8,128)(2,1)} %param.18, bf16[1,1024,1024]{1,2,0:T(8,128)(2,1)} %copy-done.3, bf16[1024,16,128]{0,2,1:T(8,128)(2,1)} %fusion.177.clone.5), kind=kOutput, calls=%fused_computation.102 | convolution fusion | flops 4301257728 | bytes 12587008 | tf_op jit(solution)/shard_map/bshre,hev->bsv/dot_general | solution.py:22
  266.0 21.1 %fusion.68 = (f32[1024]{0:T(1024)S(1)}, bf16[1,1024,1024]{1,2,0:T(8,128)(2,1)}) fusion(bf16[2,3072,1024]{2,1,0:T(8,128)(2,1)} %param.20, bf16[2,1024,3072]{2,1,0:T(8,128)(2,1)} %param.19, bf16[1,1024,1024]{1,2,0:T(8,128)(2,1)S(1)} %get-tuple-element.22, f32[1024]{0:T(1024)S(1)} %add_rsqrt_fusion.1), kind=kOutput, calls=%fused_computation.91 | convolution fusion | flops 12922649600 | bytes 18882560 | tf_op jit(solution)/shard_map/bsf,fd->bsd/dot_general | solution.py:28
  287.2 0.0 copy-start.2
  287.2 14.2 %convert_bitcast_fusion.2 = bf16[2,2,1,1024,8,128]{5,3,4,1,0,2:T(8,128)(2,1)} fusion(bf16[2,1024,2,8,128]{4,3,2,1,0:T(8,128)(2,1)} %param.24, bf16[1,1024,1024]{1,2,0:T(8,128)(2,1)} %get-tuple-element.24, f32[1024]{0:T(1024)S(1)} %add_rsqrt_fusion), kind=kOutput, calls=%fused_computation.46 | convolution fusion | flops 8597274624 | bytes 18878464 | tf_op jit(solution)/shard_map/bsd,ldtge->ltbsge/dot_general | solution.py:64
  301.4 4.0 collective-permute-start
  305.4 0.0 collective-permute-start.1
  305.4 0.0 copy-done.2
  305.4 0.1 fusion.322
  305.6 14.9 %fusion.390 = (bf16[1,1024,3,16,128]{4,3,2,1,0:T(8,128)(2,1)}, bf16[1,1024,3,16,128]{4,3,2,1,0:T(8,128)(2,1)S(1)}) fusion(bf16[2,1024,3,16,128]{4,3,2,1,0:T(8,128)(2,1)} %param.21), kind=kLoop, calls=%fused_computation.324 | loop fusion | bytes 50331648 | tf_op jit(solution)/shard_map/slice | solution.py:47
  320.5 7.3 %fusion.182 = bf16[3,1,64,16,128]{4,2,3,0,1:T(8,128)(2,1)S(1)} fusion(bf16[1,1024,3,16,128]{4,3,2,1,0:T(8,128)(2,1)S(1)} %get-tuple-element.6, bf16[1,64,1024]{2,1,0:T(8,128)(2,1)S(1)} %copy-done.2, f32[64]{0:T(128)S(1)} %add_rsqrt_fusion.10), kind=kOutput, calls=%fused_computation.178 | convolution fusion | flops 805896192 | bytes 13500672 | tf_op jit(solution)/shard_map/bsd,dthe->tbshe/dot_general | solution.py:20
  327.8 0.3 fusion.392
  328.1 0.1 fusion.312
  328.2 3.3 multiply_reduce_fusion.4
  331.6 8.6 %slice_bitcast_fusion.12 = (bf16[1024,8,2,128]{3,2,1,0:T(2,128)(2,1)}, bf16[1024,8,2,128]{3,2,1,0:T(2,128)(2,1)}) fusion(bf16[2,1024,8,2,128]{4,3,2,1,0:T(2,128)(2,1)} %param.23), kind=kLoop, calls=%fused_computation.141 | loop fusion | bytes 16777216 | tf_op jit(solution)/shard_map/squeeze | solution.py:48
  340.2 145.9 %collective-permute-done.1 = s32[1]{0:T(128)} collective-permute-done((s32[1]{0:T(128)}, s32[1]{0:T(128)}, u32[]{:S(2)}, u32[]{:S(2)}) %collective-permute-start.1) | collective-permute-done | bytes 36 | tf_op jit(solution)/shard_map/ppermute | solution.py:66
  486.1 0.6 iota_compare_fusion.1
  486.7 0.0 collective-permute-done
  486.7 6.3 %bitcast_reduce_fusion.3 = (f32[8,2,64]{2,1,0:T(2,128)S(1)}, f32[8,1024,64,2]{1,2,3,0:T(8,128)}) fusion(pred[1024]{0:T(1024)(128)(4,1)S(1)} %iota_compare_fusion.1, bf16[1024,8,2,128]{3,2,1,0:T(2,128)(2,1)} %get-tuple-element.10, f32[1,64,1024]{2,1,0:T(8,128)S(1)} %get-tuple-element.26, f32[64]{0:T(128)S(1)} %add_rsqrt_fusion.9, ...), kind=kOutput, calls=%fused_computation.130 | convolution fusion | flops 540277760 | bytes 10753280 | tf_op jit(solution)/shard_map/bqgrd,bkgd->bgrqk/dot_general | solution.py:14
  493.0 3.2 fusion.124
  496.2 6.1 %multiply_reduce_fusion.3 = (f32[64]{0:T(128)S(1)}, f32[1,64,1024]{2,1,0:T(8,128)S(1)}) fusion(f32[1,64,1024]{2,1,0:T(8,128)S(1)} %get-tuple-element.26, bf16[2,8,2,128,1024]{4,3,2,1,0:T(8,128)(2,1)} %param.25, f32[8,2,64]{2,1,0:T(2,128)S(1)} %fusion.124, f32[8,2,64]{2,1,0:T(2,128)S(1)} %get-tuple-element.27, f32[8,1024,64,2]{1,2,3,0:T(8,128)} %get-tuple-element.28, ...), kind=kOutput, calls=%fused_computation.270 | convolution fusion | flops 542572480 | bytes 11019520 | tf_op jit(solution)/shard_map/bsgre,grev->bsv/dot_general | solution.py:50
  502.3 7.2 %multiply_reduce_fusion.2 = (f32[64]{0:T(128)S(1)}, f32[1,64,1024]{2,1,0:T(8,128)S(1)}) fusion(f32[1,64,1024]{2,1,0:T(8,128)S(1)} %get-tuple-element.30, bf16[2,3072,1024]{2,1,0:T(8,128)(2,1)} %param.27, bf16[2,1024,3072]{2,1,0:T(8,128)(2,1)} %param.26, f32[64]{0:T(128)S(1)} %add_rsqrt_fusion.8), kind=kOutput, calls=%fused_computation.268 | convolution fusion | flops 807534528 | bytes 13370112 | tf_op jit(solution)/shard_map/bsf,fd->bsd/dot_general | solution.py:28
  509.6 7.0 %fusion.181 = bf16[3,1,64,16,128]{4,2,3,0,1:T(8,128)(2,1)S(1)} fusion(bf16[1,1024,3,16,128]{4,3,2,1,0:T(8,128)(2,1)} %get-tuple-element.5, f32[1,64,1024]{2,1,0:T(8,128)S(1)} %get-tuple-element.32, f32[64]{0:T(128)S(1)} %add_rsqrt_fusion.7), kind=kOutput, calls=%fused_computation.177 | convolution fusion | flops 805830656 | bytes 13631744 | tf_op jit(solution)/shard_map/bsd,dthe->tbshe/dot_general | solution.py:20
  516.6 0.3 fusion.417
  516.9 0.1 fusion.313
  517.0 3.3 multiply_reduce_fusion.1
  520.4 6.3 %bitcast_reduce_fusion.2 = (f32[8,2,64]{2,1,0:T(2,128)S(1)}, f32[8,1024,64,2]{1,2,3,0:T(8,128)}) fusion(pred[1024]{0:T(1024)(128)(4,1)S(1)} %iota_compare_fusion.1, bf16[1024,8,2,128]{3,2,1,0:T(2,128)(2,1)} %get-tuple-element.9, f32[1,64,1024]{2,1,0:T(8,128)S(1)} %get-tuple-element.36, f32[64]{0:T(128)S(1)} %add_rsqrt_fusion.6, ...), kind=kOutput, calls=%fused_computation.122 | convolution fusion | flops 540277760 | bytes 10753280 | tf_op jit(solution)/shard_map/bqgrd,bkgd->bgrqk/dot_general | solution.py:14
  526.7 3.2 fusion.125
  529.8 6.3 %multiply_reduce_fusion = (f32[64]{0:T(128)S(1)}, f32[1,64,1024]{2,1,0:T(8,128)S(1)}) fusion(f32[1,64,1024]{2,1,0:T(8,128)S(1)} %get-tuple-element.36, bf16[2,8,2,128,1024]{4,3,2,1,0:T(8,128)(2,1)} %param.25, f32[8,2,64]{2,1,0:T(2,128)S(1)} %fusion.125, f32[8,2,64]{2,1,0:T(2,128)S(1)} %get-tuple-element.37, f32[8,1024,64,2]{1,2,3,0:T(8,128)} %get-tuple-element.38, ...), kind=kOutput, calls=%fused_computation.263 | convolution fusion | flops 542572480 | bytes 11019520 | tf_op jit(solution)/shard_map/bsgre,grev->bsv/dot_general | solution.py:50
  536.1 7.8 %fusion.253 = bf16[1,64,1024]{2,1,0:T(8,128)(2,1)} fusion(f32[1,64,1024]{2,1,0:T(8,128)S(1)} %get-tuple-element.40, bf16[2,3072,1024]{2,1,0:T(8,128)(2,1)} %param.27, bf16[2,1024,3072]{2,1,0:T(8,128)(2,1)} %param.26, f32[64]{0:T(128)S(1)} %add_rsqrt_fusion.5), kind=kOutput, calls=%fused_computation.211 | convolution fusion | flops 807337984 | bytes 13238784 | tf_op jit(solution)/shard_map/bsf,fd->bsd/dot_general | solution.py:28
  (13 shorter events, 0.1 us)
Async XLA Ops:
  2.9 19.9 %copy-start = (bf16[1,1024,1024]{1,2,0:T(8,128)(2,1)}, bf16[1,1024,1024]{1,2,0:T(8,128)(2,1)S(1)}, u32[]{:S(2)}) copy-start(bf16[1,1024,1024]{1,2,0:T(8,128)(2,1)S(1)} %copy.17) | copy-start | bytes 6291460
  94.4 29.6 %copy-start.1 = (bf16[1,1024,1024]{1,2,0:T(8,128)(2,1)S(1)}, bf16[1,1024,1024]{1,2,0:T(8,128)(2,1)}, u32[]{:S(2)}) copy-start(bf16[1,1024,1024]{1,2,0:T(8,128)(2,1)} %copy-done) | copy-start | bytes 6291460
  154.5 1.4 copy-start.3
  287.2 18.3 %copy-start.2 = (bf16[1,64,1024]{2,1,0:T(8,128)(2,1)S(1)}, bf16[1,64,1024]{2,1,0:T(8,128)(2,1)}, u32[]{:S(2)}) copy-start(bf16[1,64,1024]{2,1,0:T(8,128)(2,1)} %param.16) | copy-start | bytes 393220
  301.4 185.4 %collective-permute-start = (bf16[2,2,1,1024,8,128]{5,3,4,1,0,2:T(8,128)(2,1)}, bf16[2,2,1,1024,8,128]{5,3,4,1,0,2:T(8,128)(2,1)}, u32[]{:S(2)}, u32[]{:S(2)}) collective-permute-start(bf16[2,2,1,1024,8,128]{5,3,4,1,0,2:T(8,128)(2,1)} %convert_bitcast_fusion.2), channel_id=1, source_target_pairs={{0,64},{1,65},{2,66},{3,67},{4,68},{5,69},{6,70},{7,71},{8,72},{9,... | collective-permute-start | bytes 25165832 | tf_op jit(solution)/shard_map/ppermute | solution.py:65
  305.4 180.7 %collective-permute-start.1 = (s32[1]{0:T(128)}, s32[1]{0:T(128)}, u32[]{:S(2)}, u32[]{:S(2)}) collective-permute-start(s32[1]{0:T(128)} %param.15), channel_id=1, source_target_pairs={{0,64},{1,65},{2,66},{3,67},{4,68},{5,69},{6,70},{7,71},{8,72},{9,... | collective-permute-start | bytes 20 | tf_op jit(solution)/shard_map/ppermute | solution.py:66
where the time goes:
time: 552 us; the launch traced here: 544 us
  matrix products  296 us (54%)
  waiting for transfers between devices  146 us (26%)
  other arithmetic  50.7 us (9%)
  local copies, waits for them, and re-layouts  46.5 us (8%)
    ppermute x1, waiting for transfers between devices, body(): len_recv = lax.ppermute(enc_len, 'stage', swap)  146 us
    dot_general x6, matrix products, attend(): jnp.einsum('bqgrd,bkgd->bgrqk', query, keys, preferred_element_type=jnp.f...  68.2 us
    dot_general x4, matrix products, self_block(): jnp.einsum('bsd,dthe->tbshe', rms_norm(state), w_qkv, preferred_element_t...  59.8 us
    dot_general x2, matrix products, attend(): jnp.einsum('bgrqk,bkgd->bqgrd', attn_probs, values, preferred_element_typ...  59 us
    dot_general x4, matrix products, ffn_block(): jnp.einsum('bsf,fd->bsd', hidden, w_out, preferred_element_type=jnp.float32)  57 us
    reduce_sum x6, other arithmetic, attend(): jax.nn.softmax(jnp.where(valid, scores, -1e+30), axis=-1)  49.4 us
    dot_general x4, matrix products, self_block(): jnp.einsum('bshre,hev->bsv', mixed, w_out, preferred_element_type=jnp.flo...  25.4 us
    slice x1, local copies, waits for them, and re-layouts, encoder(): state = self_block(state, enc_wqkv[layer], enc_wo[layer], valid)  18.8 us
  transfers between devices with their start and end apart: 2, of which 1 were waited for; matrix products, arithmetic and copies ran while one was open for 6% of the time, Pallas kernels for 0%

commit v1 on v0

--- a/solution.py
+++ b/solution.py
@@ -62,8 +62,8 @@
     def body(x_enc, enc_len, y, enc_wqkv, enc_wo, enc_w1, enc_w2, dec_wqkv, dec_wo, cross_wq, cross_wkv, cross_wo, dec_w1, dec_w2):
         enc_out = encoder(x_enc, enc_len, enc_wqkv, enc_wo, enc_w1, enc_w2)
         kv_all = jnp.einsum("bsd,ldtge->ltbsge", enc_out, cross_wkv, preferred_element_type=jnp.float32).astype(jnp.bfloat16)
-        kv_recv = lax.ppermute(kv_all, "stage", swap)
-        len_recv = lax.ppermute(enc_len, "stage", swap)
-        return decoder(y, kv_recv, len_recv, dec_wqkv, dec_wo, cross_wq, cross_wo, dec_w1, dec_w2)
+        y_recv = lax.ppermute(y, "stage", swap)
+        done = decoder(y_recv, kv_all, enc_len, dec_wqkv, dec_wo, cross_wq, cross_wo, dec_w1, dec_w2)
+        return lax.ppermute(done, "stage", swap)
 
     return jax.shard_map(body, mesh=mesh, in_specs=(rows, rows, rows) + (whole,) * 11, out_specs=rows, check_vma=False)

time: 552 us -> 415 us (0.75)
  waiting for transfers between devices: 146 us -> 6.46 us
    ppermute x2, waiting for transfers between devices: 146 us -> 6.46 us  [the longest x1 6.46 us: body(): return lax.ppermute(done, 'stage', swap)]
  transfers between devices with their start and end apart: 2 -> 2, of which waited for: 1 -> 1; matrix products, arithmetic and copies ran while one was open for 6% -> 80% of each run, Pallas kernels for 0% -> 0%
where the time goes in v1:
time: 415 us; the launch traced here: 407 us
  matrix products  297 us (72%)
  other arithmetic  51.2 us (12%)
  local copies, waits for them, and re-layouts  47.1 us (11%)
  waiting for transfers between devices  6.46 us (2%)
    dot_general x6, matrix products, attend(): jnp.einsum('bqgrd,bkgd->bgrqk', query, keys, preferred_element_type=jnp.f...  68.1 us
    dot_general x4, matrix products, self_block(): jnp.einsum('bsd,dthe->tbshe', rms_norm(state), w_qkv, preferred_element_t...  60.9 us
    dot_general x2, matrix products, attend(): jnp.einsum('bgrqk,bkgd->bqgrd', attn_probs, values, preferred_element_typ...  59.1 us
    dot_general x4, matrix products, ffn_block(): jnp.einsum('bsf,fd->bsd', hidden, w_out, preferred_element_type=jnp.float32)  56.5 us
    reduce_sum x6, other arithmetic, attend(): jax.nn.softmax(jnp.where(valid, scores, -1e+30), axis=-1)  49.6 us
    dot_general x4, matrix products, self_block(): jnp.einsum('bshre,hev->bsv', mixed, w_out, preferred_element_type=jnp.flo...  25.4 us
    slice x1, local copies, waits for them, and re-layouts, encoder(): state = self_block(state, enc_wqkv[layer], enc_wo[layer], valid)  18.8 us
    slice x1, local copies, waits for them, and re-layouts, decoder(): state = self_block(state, dec_wqkv[layer], dec_wo[layer], causal)  15.1 us
  transfers between devices with their start and end apart: 2, of which 1 were waited for; matrix products, arithmetic and copies ran while one was open for 80% of the time, Pallas kernels for 0%

profile of v1, /device:TPU:0, one launch (start us, length us, event | category | flops | bytes accessed | tf_op | source)
XLA Modules:
  0.0 407.0 jit_solution(15760064416477422977)
XLA Ops:
  0.0 4.0 collective-permute-start
  4.7 2.9 copy.17
  7.6 0.0 copy-start
  7.6 0.5 fusion.70
  8.1 18.8 %fusion.391 = (bf16[1,1024,3,16,128]{4,3,2,1,0:T(8,128)(2,1)}, bf16[1,1024,3,16,128]{4,3,2,1,0:T(8,128)(2,1)}) fusion(bf16[2,1024,3,16,128]{4,3,2,1,0:T(8,128)(2,1)} %param.17), kind=kLoop, calls=%fused_computation.324 | loop fusion | bytes 50331648 | tf_op jit(solution)/shard_map/slice | solution.py:36
  26.8 0.0 copy-done
  26.8 22.7 %convert_bitcast_fusion.1 = bf16[3,1,1024,16,128]{4,2,3,0,1:T(8,128)(2,1)} fusion(bf16[1,1024,3,16,128]{4,3,2,1,0:T(8,128)(2,1)} %get-tuple-element.8, bf16[1,1024,1024]{1,2,0:T(8,128)(2,1)S(1)} %copy.17, f32[1024]{0:T(1024)S(1)} %add_rsqrt_fusion.4), kind=kOutput, calls=%fused_computation.43 | convolution fusion | flops 12894339072 | bytes 27267072 | tf_op jit(solution)/shard_map/bsd,dthe->tbshe/dot_general | solution.py:20
  49.5 27.4 %bitcast_reduce_fusion.1 = (f32[16,1024]{1,0:T(8,128)S(1)}, f32[16,1024,1024]{2,1,0:T(8,128)}) fusion(pred[1024]{0:T(1024)(128)(4,1)S(1)} %iota_compare_fusion.1, bf16[3,1,1024,16,128]{4,2,3,0,1:T(8,128)(2,1)} %convert_bitcast_fusion.1), kind=kOutput, calls=%fused_computation.5 | convolution fusion | flops 4345282560 | bytes 75564032 | tf_op jit(solution)/shard_map/bqgrd,bkgd->bgrqk/dot_general | solution.py:14
  76.9 21.4 %fusion.2 = f32[16,1024]{1,0:T(8,128)S(1)} fusion(f32[16,1024,1024]{2,1,0:T(8,128)} %get-tuple-element.14, f32[16,1024]{1,0:T(8,128)S(1)} %get-tuple-element.13, pred[1024]{0:T(1024)(128)(4,1)S(1)} %iota_compare_fusion.1), kind=kLoop, calls=%fused_computation.10 | loop fusion | flops 67092480 | bytes 67240960 | tf_op jit(solution)/shard_map/reduce_sum | solution.py:15
  98.4 0.0 copy-start.1
  98.4 29.7 %fusion.171.clone.5 = bf16[1024,16,128]{0,2,1:T(8,128)(2,1)} fusion(f32[16,1024]{1,0:T(8,128)S(1)} %fusion.2, f32[16,1024]{1,0:T(8,128)S(1)} %get-tuple-element.13, f32[16,1024,1024]{2,1,0:T(8,128)} %get-tuple-element.14, pred[1024]{0:T(1024)(128)(4,1)S(1)} %iota_compare_fusion.1, ...), kind=kOutput, calls=%fused_computation.118.clone.clone.clone.clone.clone.2 | convolution fusion | flops 4380950528 | bytes 75629568 | tf_op jit(solution)/shard_map/bgrqk,bkgd->bqgrd/dot_general | solution.py:16
  128.1 0.0 copy-done.1
  128.1 9.8 %fusion.73 = (f32[1024]{0:T(1024)S(1)}, bf16[1,1024,1024]{1,2,0:T(8,128)(2,1)}) fusion(bf16[2,16,128,1024]{3,2,1,0:T(8,128)(2,1)} %param.18, bf16[1,1024,1024]{1,2,0:T(8,128)(2,1)S(1)} %copy-done.1, bf16[1024,16,128]{0,2,1:T(8,128)(2,1)} %fusion.171.clone.5), kind=kOutput, calls=%fused_computation.96 | convolution fusion | flops 4301257728 | bytes 12587008 | tf_op jit(solution)/shard_map/bshre,hev->bsv/dot_general | solution.py:22
  137.8 20.9 %fusion.76 = (f32[1024]{0:T(1024)S(1)}, bf16[1,1024,1024]{1,2,0:T(8,128)(2,1)S(1)}) fusion(bf16[2,3072,1024]{2,1,0:T(8,128)(2,1)} %param.20, bf16[2,1024,3072]{2,1,0:T(8,128)(2,1)} %param.19, bf16[1,1024,1024]{1,2,0:T(8,128)(2,1)} %get-tuple-element.16, f32[1024]{0:T(1024)S(1)} %add_rsqrt_fusion.3), kind=kOutput, calls=%fused_computation.99 | convolution fusion | flops 12922649600 | bytes 18882560 | tf_op jit(solution)/shard_map/bsf,fd->bsd/dot_general | solution.py:28
  158.8 0.0 copy-start.2
  158.8 1.3 copy-done.2
  160.1 22.7 %convert_bitcast_fusion = bf16[3,1,1024,16,128]{4,2,3,0,1:T(8,128)(2,1)} fusion(bf16[1,1024,3,16,128]{4,3,2,1,0:T(8,128)(2,1)} %get-tuple-element.7, bf16[1,1024,1024]{1,2,0:T(8,128)(2,1)S(1)} %get-tuple-element.18, f32[1024]{0:T(1024)S(1)} %add_rsqrt_fusion.2), kind=kOutput, calls=%fused_computation.42 | convolution fusion | flops 12894339072 | bytes 27267072 | tf_op jit(solution)/shard_map/bsd,dthe->tbshe/dot_general | solution.py:20
  182.8 27.6 %bitcast_reduce_fusion = (f32[16,1024]{1,0:T(8,128)S(1)}, f32[16,1024,1024]{2,1,0:T(8,128)}) fusion(pred[1024]{0:T(1024)(128)(4,1)S(1)} %iota_compare_fusion.1, bf16[3,1,1024,16,128]{4,2,3,0,1:T(8,128)(2,1)} %convert_bitcast_fusion), kind=kOutput, calls=%fused_computation.1 | convolution fusion | flops 4345282560 | bytes 75564032 | tf_op jit(solution)/shard_map/bqgrd,bkgd->bgrqk/dot_general | solution.py:14
  210.4 21.4 %fusion.3 = f32[16,1024]{1,0:T(8,128)S(1)} fusion(f32[16,1024,1024]{2,1,0:T(8,128)} %get-tuple-element.20, f32[16,1024]{1,0:T(8,128)S(1)} %get-tuple-element.19, pred[1024]{0:T(1024)(128)(4,1)S(1)} %iota_compare_fusion.1), kind=kLoop, calls=%fused_computation.11 | loop fusion | flops 67092480 | bytes 67240960 | tf_op jit(solution)/shard_map/reduce_sum | solution.py:15
  231.9 29.4 %fusion.177.clone.5 = bf16[1024,16,128]{0,2,1:T(8,128)(2,1)} fusion(f32[16,1024]{1,0:T(8,128)S(1)} %fusion.3, f32[16,1024]{1,0:T(8,128)S(1)} %get-tuple-element.19, f32[16,1024,1024]{2,1,0:T(8,128)} %get-tuple-element.20, pred[1024]{0:T(1024)(128)(4,1)S(1)} %iota_compare_fusion.1, ...), kind=kOutput, calls=%fused_computation.117.clone.clone.clone.clone.clone.2 | convolution fusion | flops 4380950528 | bytes 75629568 | tf_op jit(solution)/shard_map/bgrqk,bkgd->bqgrd/dot_general | solution.py:16
  261.3 9.0 %fusion.79 = (f32[1024]{0:T(1024)S(1)}, bf16[1,1024,1024]{1,2,0:T(8,128)(2,1)S(1)}) fusion(bf16[2,16,128,1024]{3,2,1,0:T(8,128)(2,1)} %param.18, bf16[1,1024,1024]{1,2,0:T(8,128)(2,1)} %copy-done.2, bf16[1024,16,128]{0,2,1:T(8,128)(2,1)} %fusion.177.clone.5), kind=kOutput, calls=%fused_computation.102 | convolution fusion | flops 4301257728 | bytes 12587008 | tf_op jit(solution)/shard_map/bshre,hev->bsv/dot_general | solution.py:22
  270.3 21.1 %fusion.68 = (f32[1024]{0:T(1024)S(1)}, bf16[1,1024,1024]{1,2,0:T(8,128)(2,1)}) fusion(bf16[2,3072,1024]{2,1,0:T(8,128)(2,1)} %param.20, bf16[2,1024,3072]{2,1,0:T(8,128)(2,1)} %param.19, bf16[1,1024,1024]{1,2,0:T(8,128)(2,1)S(1)} %get-tuple-element.22, f32[1024]{0:T(1024)S(1)} %add_rsqrt_fusion.1), kind=kOutput, calls=%fused_computation.91 | convolution fusion | flops 12922649600 | bytes 18882560 | tf_op jit(solution)/shard_map/bsf,fd->bsd/dot_general | solution.py:28
  291.4 0.0 copy-start.3
  291.4 15.1 %fusion.390 = (bf16[1,1024,3,16,128]{4,3,2,1,0:T(8,128)(2,1)}, bf16[1,1024,3,16,128]{4,3,2,1,0:T(8,128)(2,1)S(1)}) fusion(bf16[2,1024,3,16,128]{4,3,2,1,0:T(8,128)(2,1)} %param.21), kind=kLoop, calls=%fused_computation.323 | loop fusion | bytes 50331648 | tf_op jit(solution)/shard_map/slice | solution.py:47
  306.5 0.0 copy-done.3
  306.5 14.9 %convert_bitcast_fusion.2 = bf16[2,2,1,1024,8,128]{5,3,4,1,0,2:T(8,128)(2,1)} fusion(bf16[2,1024,2,8,128]{4,3,2,1,0:T(8,128)(2,1)} %param.24, bf16[1,1024,1024]{1,2,0:T(8,128)(2,1)S(1)} %copy-done.3, f32[1024]{0:T(1024)S(1)} %add_rsqrt_fusion), kind=kOutput, calls=%fused_computation.46 | convolution fusion | flops 8597274624 | bytes 18878464 | tf_op jit(solution)/shard_map/bsd,ldtge->ltbsge/dot_general | solution.py:64
  321.3 8.4 %slice_bitcast_fusion.12 = (bf16[1024,8,2,128]{3,2,1,0:T(2,128)(2,1)}, bf16[1024,8,2,128]{3,2,1,0:T(2,128)(2,1)}) fusion(bf16[2,1024,8,2,128]{4,3,2,1,0:T(2,128)(2,1)} %param.23), kind=kLoop, calls=%fused_computation.141 | loop fusion | bytes 16777216 | tf_op jit(solution)/shard_map/squeeze | solution.py:48
  329.8 0.0 collective-permute-done
  329.8 1.0 fusion.322
  330.9 8.4 %fusion.182 = bf16[3,1,64,16,128]{4,2,3,0,1:T(8,128)(2,1)S(1)} fusion(bf16[1,1024,3,16,128]{4,3,2,1,0:T(8,128)(2,1)S(1)} %get-tuple-element.6, bf16[1,64,1024]{2,1,0:T(8,128)(2,1)} %collective-permute-done, f32[64]{0:T(128)S(1)} %add_rsqrt_fusion.10), kind=kOutput, calls=%fused_computation.178 | convolution fusion | flops 805896192 | bytes 13500672 | tf_op jit(solution)/shard_map/bsd,dthe->tbshe/dot_general | solution.py:20
  339.3 0.3 fusion.392
  339.6 0.1 fusion.312
  339.7 3.3 multiply_reduce_fusion.4
  343.1 6.3 %bitcast_reduce_fusion.3 = (f32[8,2,64]{2,1,0:T(2,128)S(1)}, f32[8,1024,64,2]{1,2,3,0:T(8,128)}) fusion(pred[1024]{0:T(1024)(128)(4,1)S(1)} %iota_compare_fusion.1, bf16[1024,8,2,128]{3,2,1,0:T(2,128)(2,1)} %get-tuple-element.10, f32[1,64,1024]{2,1,0:T(8,128)S(1)} %get-tuple-element.26, f32[64]{0:T(128)S(1)} %add_rsqrt_fusion.9, ...), kind=kOutput, calls=%fused_computation.130 | convolution fusion | flops 540277760 | bytes 10753280 | tf_op jit(solution)/shard_map/bqgrd,bkgd->bgrqk/dot_general | solution.py:14
  349.3 3.2 fusion.124
  352.5 6.0 %multiply_reduce_fusion.3 = (f32[64]{0:T(128)S(1)}, f32[1,64,1024]{2,1,0:T(8,128)S(1)}) fusion(f32[1,64,1024]{2,1,0:T(8,128)S(1)} %get-tuple-element.26, bf16[2,8,2,128,1024]{4,3,2,1,0:T(8,128)(2,1)} %param.25, f32[8,2,64]{2,1,0:T(2,128)S(1)} %fusion.124, f32[8,2,64]{2,1,0:T(2,128)S(1)} %get-tuple-element.27, f32[8,1024,64,2]{1,2,3,0:T(8,128)} %get-tuple-element.28, ...), kind=kOutput, calls=%fused_computation.270 | convolution fusion | flops 542572480 | bytes 11019520 | tf_op jit(solution)/shard_map/bsgre,grev->bsv/dot_general | solution.py:50
  358.6 7.3 %multiply_reduce_fusion.2 = (f32[64]{0:T(128)S(1)}, f32[1,64,1024]{2,1,0:T(8,128)S(1)}) fusion(f32[1,64,1024]{2,1,0:T(8,128)S(1)} %get-tuple-element.30, bf16[2,3072,1024]{2,1,0:T(8,128)(2,1)} %param.27, bf16[2,1024,3072]{2,1,0:T(8,128)(2,1)} %param.26, f32[64]{0:T(128)S(1)} %add_rsqrt_fusion.8), kind=kOutput, calls=%fused_computation.268 | convolution fusion | flops 807534528 | bytes 13370112 | tf_op jit(solution)/shard_map/bsf,fd->bsd/dot_general | solution.py:28
  365.9 7.0 %fusion.181 = bf16[3,1,64,16,128]{4,2,3,0,1:T(8,128)(2,1)S(1)} fusion(bf16[1,1024,3,16,128]{4,3,2,1,0:T(8,128)(2,1)} %get-tuple-element.5, f32[1,64,1024]{2,1,0:T(8,128)S(1)} %get-tuple-element.32, f32[64]{0:T(128)S(1)} %add_rsqrt_fusion.7), kind=kOutput, calls=%fused_computation.177 | convolution fusion | flops 805830656 | bytes 13631744 | tf_op jit(solution)/shard_map/bsd,dthe->tbshe/dot_general | solution.py:20
  372.9 0.3 fusion.417
  373.2 0.1 fusion.313
  373.3 3.3 multiply_reduce_fusion.1
  376.6 6.3 %bitcast_reduce_fusion.2 = (f32[8,2,64]{2,1,0:T(2,128)S(1)}, f32[8,1024,64,2]{1,2,3,0:T(8,128)}) fusion(pred[1024]{0:T(1024)(128)(4,1)S(1)} %iota_compare_fusion.1, bf16[1024,8,2,128]{3,2,1,0:T(2,128)(2,1)} %get-tuple-element.9, f32[1,64,1024]{2,1,0:T(8,128)S(1)} %get-tuple-element.36, f32[64]{0:T(128)S(1)} %add_rsqrt_fusion.6, ...), kind=kOutput, calls=%fused_computation.122 | convolution fusion | flops 540277760 | bytes 10753280 | tf_op jit(solution)/shard_map/bqgrd,bkgd->bgrqk/dot_general | solution.py:14
  382.9 3.4 fusion.125
  386.3 6.1 %multiply_reduce_fusion = (f32[64]{0:T(128)S(1)}, f32[1,64,1024]{2,1,0:T(8,128)S(1)}) fusion(f32[1,64,1024]{2,1,0:T(8,128)S(1)} %get-tuple-element.36, bf16[2,8,2,128,1024]{4,3,2,1,0:T(8,128)(2,1)} %param.25, f32[8,2,64]{2,1,0:T(2,128)S(1)} %fusion.125, f32[8,2,64]{2,1,0:T(2,128)S(1)} %get-tuple-element.37, f32[8,1024,64,2]{1,2,3,0:T(8,128)} %get-tuple-element.38, ...), kind=kOutput, calls=%fused_computation.263 | convolution fusion | flops 542572480 | bytes 11019520 | tf_op jit(solution)/shard_map/bsgre,grev->bsv/dot_general | solution.py:50
  392.4 7.2 %fusion.253 = bf16[1,64,1024]{2,1,0:T(8,128)(2,1)S(1)} fusion(f32[1,64,1024]{2,1,0:T(8,128)S(1)} %get-tuple-element.40, bf16[2,3072,1024]{2,1,0:T(8,128)(2,1)} %param.27, bf16[2,1024,3072]{2,1,0:T(8,128)(2,1)} %param.26, f32[64]{0:T(128)S(1)} %add_rsqrt_fusion.5), kind=kOutput, calls=%fused_computation.211 | convolution fusion | flops 807337984 | bytes 13238784 | tf_op jit(solution)/shard_map/bsf,fd->bsd/dot_general | solution.py:28
  399.5 0.1 collective-permute-start.1
  399.6 6.5 %collective-permute-done.1 = bf16[1,64,1024]{2,1,0:T(8,128)(2,1)S(1)} collective-permute-done((bf16[1,64,1024]{2,1,0:T(8,128)(2,1)S(1)}, bf16[1,64,1024]{2,1,0:T(8,128)(2,1)S(1)}, u32[]{:S(2)}, u32[]{:S(2)}) %collective-permute-start.1) | collective-permute-done | bytes 131104 | tf_op jit(solution)/shard_map/ppermute | solution.py:67
  406.1 0.7 copy.108
  (13 shorter events, 0.1 us)
Async XLA Ops:
  0.0 329.8 %collective-permute-start = (bf16[1,64,1024]{2,1,0:T(8,128)(2,1)}, bf16[1,64,1024]{2,1,0:T(8,128)(2,1)}, u32[]{:S(2)}, u32[]{:S(2)}) collective-permute-start(bf16[1,64,1024]{2,1,0:T(8,128)(2,1)} %param.16), channel_id=1, source_target_pairs={{0,64},{1,65},{2,66},{3,67},{4,68},{5,69},{6,70},{7,71},{8,72},{9,... | collective-permute-start | bytes 393224 | tf_op jit(solution)/shard_map/ppermute | solution.py:65
  7.6 19.3 %copy-start = (bf16[1,1024,1024]{1,2,0:T(8,128)(2,1)}, bf16[1,1024,1024]{1,2,0:T(8,128)(2,1)S(1)}, u32[]{:S(2)}) copy-start(bf16[1,1024,1024]{1,2,0:T(8,128)(2,1)S(1)} %copy.17) | copy-start | bytes 6291460
  98.4 29.7 %copy-start.1 = (bf16[1,1024,1024]{1,2,0:T(8,128)(2,1)S(1)}, bf16[1,1024,1024]{1,2,0:T(8,128)(2,1)}, u32[]{:S(2)}) copy-start(bf16[1,1024,1024]{1,2,0:T(8,128)(2,1)} %copy-done) | copy-start | bytes 6291460
  158.8 1.4 copy-start.2
  291.4 15.1 %copy-start.3 = (bf16[1,1024,1024]{1,2,0:T(8,128)(2,1)S(1)}, bf16[1,1024,1024]{1,2,0:T(8,128)(2,1)}, u32[]{:S(2)}) copy-start(bf16[1,1024,1024]{1,2,0:T(8,128)(2,1)} %get-tuple-element.24) | copy-start | bytes 6291460
  399.5 6.5 %collective-permute-start.1 = (bf16[1,64,1024]{2,1,0:T(8,128)(2,1)S(1)}, bf16[1,64,1024]{2,1,0:T(8,128)(2,1)S(1)}, u32[]{:S(2)}, u32[]{:S(2)}) collective-permute-start(bf16[1,64,1024]{2,1,0:T(8,128)(2,1)S(1)} %fusion.253), channel_id=1, source_target_pairs={{0,64},{1,65},{2,66},{3,67},{4,68},{5,69},{6,70},{7,71},{8,72},{9,... | collective-permute-start | bytes 393224 | tf_op jit(solution)/shard_map/ppermute | solution.py:67

commit v2 on v1

v2 whole, which is shorter than its diff:
```python
import jax
import jax.numpy as jnp
from jax import lax
from jax.experimental import pallas as pl
from jax.experimental.pallas import tpu as pltpu
from jax.sharding import PartitionSpec as P

F32, BF16 = jnp.float32, jnp.bfloat16
NT = (((1,), (1,)), ((), ()))
SCORE = 128 ** -0.5 * 1.4426950408889634
TQ = 256
RB = 256
FC = 1024


def rms_norm(inputs):
    wide = inputs.astype(F32)
    return (wide * lax.rsqrt(jnp.mean(wide * wide, axis=-1, keepdims=True) + 1e-6)).astype(BF16)


def matmul(a, b):
    return jnp.dot(a, b, preferred_element_type=F32)


def probs(s):
    top = jnp.max(s, axis=1, keepdims=True) * SCORE
    e = jnp.exp2(s * SCORE - top)
    return (e * (1.0 / jnp.sum(e, axis=1, keepdims=True))).astype(BF16)


def project8(z_ref, w_ref, half, stage, write):
    rows = pl.ds(pl.multiple_of(half * 8, 8), 8)
    for c in range(4):
        stage[c] = w_ref[c * 256:(c + 1) * 256, rows, :].astype(F32).reshape(256 * 8, 128)
    for h in range(0, 8, 2):
        w = jnp.concatenate([
            jnp.concatenate([stage[c, pl.ds(h + u, 256, stride=8), :].astype(BF16) for u in range(2)], axis=1)
            for c in range(4)], axis=0)
        write(h * 128, matmul(z_ref[...], w).astype(BF16))


def row_kernel(len_ref, y_ref, x, e_qkv, e_o, e_1, e_2, d_qkv, d_o, c_q, c_kv, c_o, d_1, d_2, o_ref,
               state, xn, qkv, stage, b_qkv, b_o, b_cq, b_co, b_1, b_2, proj, mix, st, z, sems):
    n, m = state.shape[0], y_ref.shape[0]
    enc, dec = (e_qkv, e_o, e_1, e_2), (d_qkv, d_o, d_1, d_2)

    def copy(which, l, i):
        src = which[0].at[l, :, i] if not isinstance(i, int) or i < 3 else which[i - 2].at[l]
        dst = b_qkv.at[i] if not isinstance(i, int) or i < 3 else (b_o, b_1, b_2)[i - 3]
        return pltpu.make_async_copy(src, dst, sems.at[i])

    def co_copy(l):
        return pltpu.make_async_copy(c_o.at[l], b_co, sems.at[6])

    def cq_copy(l):
        return pltpu.make_async_copy(c_q.at[l], b_cq, sems.at[7])

    def kv_copy(j):
        slot = lax.rem(j, 2)
        return pltpu.make_async_copy(c_kv.at[j // 2, :, lax.rem(j, 2)],
                                     b_cq.at[:, pl.ds(pl.multiple_of(slot * 8, 8), 8)], sems.at[8 + slot])

    x_copy = pltpu.make_async_copy(x, state, sems.at[10])
    x_copy.start()
    for i in range(3):
        copy(enc, 0, i).start()
    st[...] = y_ref[...]
    row = lax.broadcasted_iota(jnp.int32, (n, 128), 0)
    lane = lax.broadcasted_iota(jnp.int32, (n, 128), 1)
    bias = jnp.where((row >= len_ref[0]) & (lane == 0), -1e30, 0.0).astype(BF16)
    one = jnp.where(lax.broadcasted_iota(jnp.int32, (TQ, 128), 1) == 0, 1.0, 0.0).astype(BF16)
    x_copy.wait()
    for r in range(0, n, RB):
        xn[r:r + RB] = rms_norm(state[r:r + RB])
    for i in range(3, 6):
        copy(enc, 0, i).start()
    co_copy(0).start()
    kv_copy(jnp.int32(0)).start()
    kv_copy(jnp.int32(1)).start()

    def enc_layer(l, _):
        def refill(i):
            @pl.when(l == 0)
            def _():
                copy(enc, 1, i).start()

            @pl.when(l == 1)
            def _():
                copy(dec, 0, i).start()

        def qkv_step(j, _):
            t, half = j // 2, lax.rem(j, 2)

            @pl.when(half == 0)
            def _():
                copy(enc, 0, t).wait()

            def write(col, value):
                qkv[j, :, col:col + 256] = value

            project8(xn, b_qkv.at[t], half, stage, write)

            @pl.when(half == 1)
            def _():
                refill(t)

            return 0

        lax.fori_loop(0, 6, qkv_step, 0)

        def attn_step(j, _):
            half, base = j // 4, lax.rem(j, 4) * 256
            work = [(h, i) for h in range(2) for i in range(n // TQ)]

            def cols(h):
                return pl.ds(pl.multiple_of(base + h * 128, 128), 128)

            def score(item):
                h, i = item
                keys = jnp.concatenate([qkv[2 + half, :, cols(h)], bias], axis=1)
                query = jnp.concatenate([qkv[half, i * TQ:(i + 1) * TQ, cols(h)], one], axis=1)
                return lax.dot_general(query, keys, NT, preferred_element_type=F32)

            s = score(work[0])
            for k, (h, i) in enumerate(work):
                ahead = score(work[k + 1]) if k + 1 < len(work) else None
                qkv[half, i * TQ:(i + 1) * TQ, cols(h)] = matmul(probs(s), qkv[4 + half, :, cols(h)]).astype(BF16)
                s = ahead
            return 0

        lax.fori_loop(0, 8, attn_step, 0)

        for i in range(3, 6):
            copy(enc, 0, i).wait()

        def ffn_step(j, _):
            rs = pl.ds(pl.multiple_of(j * RB, RB), RB)
            mixed = jnp.concatenate([qkv[0, rs, :], qkv[1, rs, :]], axis=1)
            mid = (state[rs, :].astype(F32) + matmul(mixed, b_o[...])).astype(BF16)
            normed = rms_norm(mid)
            total = mid.astype(F32)
            u = matmul(normed, b_1[:, 0:FC])
            for c in range(0, 3072, FC):
                ahead = matmul(normed, b_1[:, c + FC:c + 2 * FC]) if c + FC < 3072 else None
                total += matmul(jax.nn.gelu(u).astype(BF16), b_2[c:c + FC, :])
                u = ahead
            done = total.astype(BF16)
            state[rs, :] = done
            xn[rs, :] = rms_norm(done)
            return 0

        lax.fori_loop(0, n // RB, ffn_step, 0)
        for i in range(3, 6):
            refill(i)
        return 0

    lax.fori_loop(0, 2, enc_layer, 0)

    def kv_step(j, _):
        kv_copy(j).wait()

        def write(col, value):
            qkv[j, :, col:col + 256] = value

        project8(xn, b_cq, lax.rem(j, 2), stage, write)

        @pl.when(j < 2)
        def _():
            kv_copy(j + 2).start()

        return 0

    lax.fori_loop(0, 4, kv_step, 0)
    cq_copy(0).start()

    causal = lax.broadcasted_iota(jnp.int32, (m, m), 1) <= lax.broadcasted_iota(jnp.int32, (m, m), 0)
    causal = jnp.concatenate([causal] * 16, axis=0)

    def dec_layer(l, _):
        def again(start):
            @pl.when(l == 0)
            def _():
                start()

        z[...] = rms_norm(st[...])

        def qkv_step(j, _):
            t, half = j // 2, lax.rem(j, 2)

            @pl.when(half == 0)
            def _():
                copy(dec, 0, t).wait()

            def write(col, value):
                proj[t, :, pl.ds(pl.multiple_of(half * 1024 + col, 256), 256)] = value

            project8(z, b_qkv.at[t], half, stage, write)

            @pl.when((half == 1) & (l == 0))
            def _():
                copy(dec, 1, t).start()

            return 0

        lax.fori_loop(0, 6, qkv_step, 0)
        heads = [slice(h * 128, (h + 1) * 128) for h in range(16)]
        s = [lax.dot_general(proj[0, :, hs], proj[1, :, hs], NT, preferred_element_type=F32) for hs in heads]
        p = probs(jnp.where(causal, jnp.concatenate(s, axis=0), -1e30))
        o = [matmul(p[i * m:(i + 1) * m], proj[2, :, hs]) for i, hs in enumerate(heads)]
        mix[...] = jnp.concatenate(o, axis=1).astype(BF16)
        copy(dec, 0, 3).wait()
        st[...] = (st[...].astype(F32) + matmul(mix[...], b_o[...])).astype(BF16)
        again(lambda: copy(dec, 1, 3).start())
        z[...] = rms_norm(st[...])
        cq_copy(0).wait()

        def cq_step(half, _):
            def write(col, value):
                proj[0, :, pl.ds(pl.multiple_of(half * 1024 + col, 256), 256)] = value

            project8(z, b_cq, half, stage, write)
            return 0

        lax.fori_loop(0, 2, cq_step, 0)
        again(lambda: cq_copy(1).start())
        for base in (0, 4):
            s = []
            for g in range(base, base + 4):
                q = jnp.concatenate([proj[0, :, heads[2 * g + r]] for r in range(2)], axis=0)
                s.append(lax.dot_general(jnp.concatenate([q, one[:2 * m]], axis=1),
                                         jnp.concatenate([qkv[2 * l, :, heads[g]], bias], axis=1), NT,
                                         preferred_element_type=F32))
            p = [probs(part) for part in s]
            for i in range(4):
                g = base + i
                o = matmul(p[i], qkv[2 * l + 1, :, heads[g]]).astype(BF16)
                for r in range(2):
                    mix[:, heads[2 * g + r]] = o[r * m:(r + 1) * m]
        co_copy(0).wait()
        st[...] = (st[...].astype(F32) + matmul(mix[...], b_co[...])).astype(BF16)
        again(lambda: co_copy(1).start())
        copy(dec, 0, 4).wait()
        hidden = jax.nn.gelu(matmul(rms_norm(st[...]), b_1[...])).astype(BF16)
        again(lambda: copy(dec, 1, 4).start())
        copy(dec, 0, 5).wait()
        st[...] = (st[...].astype(F32) + matmul(hidden, b_2[...])).astype(BF16)
        again(lambda: copy(dec, 1, 5).start())
        return 0

    lax.fori_loop(0, 2, dec_layer, 0)
    o_ref[...] = st[...]


def local(x_enc, enc_len, y, enc_wqkv, enc_wo, enc_w1, enc_w2, dec_wqkv, dec_wo, cross_wq, cross_wkv, cross_wo, dec_w1, dec_w2):
    n, m = x_enc.shape[1], y.shape[1]
    vmem = pl.BlockSpec(memory_space=pltpu.VMEM)
    flat = lambda w: w.reshape(2, 2048, 1024)
    return pl.pallas_call(
        row_kernel,
        in_specs=[pl.BlockSpec(memory_space=pltpu.SMEM), vmem] + [pl.BlockSpec(memory_space=pl.ANY)] * 12,
        out_specs=vmem,
        out_shape=jax.ShapeDtypeStruct((m, 1024), BF16),
        scratch_shapes=[
            pltpu.VMEM((n, 1024), BF16), pltpu.VMEM((n, 1024), BF16), pltpu.VMEM((6, n, 1024), BF16),
            pltpu.VMEM((4, 2048, 128), F32), pltpu.VMEM((3, 1024, 16, 128), BF16), pltpu.VMEM((2048, 1024), BF16),
            pltpu.VMEM((1024, 16, 128), BF16), pltpu.VMEM((2048, 1024), BF16),
            pltpu.VMEM((1024, 3072), BF16), pltpu.VMEM((3072, 1024), BF16),
            pltpu.VMEM((3, m, 2048), BF16), pltpu.VMEM((m, 2048), BF16), pltpu.VMEM((m, 1024), BF16),
            pltpu.VMEM((m, 1024), BF16), pltpu.SemaphoreType.DMA((11,)),
        ],
        compiler_params=pltpu.CompilerParams(vmem_limit_bytes=67_000_000),
        name="row",
    )(enc_len, y[0], x_enc[0], enc_wqkv, flat(enc_wo), enc_w1, enc_w2, dec_wqkv, flat(dec_wo),
      cross_wq.reshape(2, 1024, 16, 128), cross_wkv, flat(cross_wo), dec_w1, dec_w2)[None]


def solution(mesh):
    stages = mesh.shape["stage"]
    swap = [(source, (source + stages // 2) % stages) for source in range(stages)]
    rows = P(("data", "stage"))
    whole = P()

    def body(x_enc, enc_len, y, *weights):
        done = local(x_enc, enc_len, lax.ppermute(y, "stage", swap), *weights)
        return lax.ppermute(done, "stage", swap)

    return jax.shard_map(body, mesh=mesh, in_specs=(rows, rows, rows) + (whole,) * 11, out_specs=rows, check_vma=False)
```

time: 415 us -> 204 us (0.49); the launches traced: 407 us -> 204 us
  matrix products: 297 us -> 0 us
  Pallas kernels: 0 us -> 189 us
  other arithmetic: 51.2 us -> 0 us
  local copies, waits for them, and re-layouts: 47.1 us -> 0.66 us
    dot_general x23 -> x0, matrix products: 297 us -> none  [the longest x6 68.1 us: attend(): jnp.einsum('bqgrd,bkgd->bgrqk', query, keys, preferred_element_type=jnp.f...]
    pallas_call x0 -> x1, Pallas kernels: none -> 189 us  [local(): pl.pallas_call(row_kernel, in_specs=[pl.BlockSpec(memory_space=pltpu.SMEM...]
    reduce_sum x8 -> x0, other arithmetic: 51.1 us -> none  [the longest x6 49.6 us: attend(): jax.nn.softmax(jnp.where(valid, scores, -1e+30), axis=-1)]
    slice x2 -> x0, local copies, waits for them, and re-layouts: 33.8 us -> none  [the longest x1 18.8 us: encoder(): state = self_block(state, enc_wqkv[layer], enc_wo[layer], valid)]
    squeeze x1 -> x0, local copies, waits for them, and re-layouts: 8.45 us -> none  [decoder(): cross_wq[layer]]
    unnamed x10 -> x1, local copies, waits for them, and re-layouts: 4.87 us -> 0.66 us
  transfers between devices with their start and end apart: 2 -> 2, of which waited for: 1 -> 2; matrix products, arithmetic and copies ran while one was open for 80% -> 0% of each run, Pallas kernels for 0% -> 0%
where the time goes in v2:
time: 204 us
  Pallas kernels  189 us (93%)
  starting transfers between devices  7.4 us (4%)
  waiting for transfers between devices  6.34 us (3%)
    pallas_call x1, Pallas kernels, local(): pl.pallas_call(row_kernel, in_specs=[pl.BlockSpec(memory_space=pltpu.SMEM...  189 us
  transfers between devices with their start and end apart: 2, of which 2 were waited for; matrix products, arithmetic and copies ran while one was open for 0% of the time, Pallas kernels for 0%

profile of v2, /device:TPU:0, one launch (start us, length us, event | category | flops | bytes accessed | tf_op | source)
XLA Modules:
  0.0 204.3 jit_solution(8345857844204103163)
XLA Ops:
  0.0 4.0 %collective-permute-start = (bf16[1,64,1024]{2,1,0:T(8,128)(2,1)}, bf16[1,64,1024]{2,1,0:T(8,128)(2,1)}, u32[]{:S(2)}, u32[]{:S(2)}) collective-permute-start(bf16[1,64,1024]{2,1,0:T(8,128)(2,1)} %param.16), channel_id=1, source_target_pairs={{0,64},{1,65},{2,66},{3,67},{4,68},{5,69},{6,70},{7,71},{8,72},{9,... | collective-permute-start | bytes 393224 | tf_op jit(solution)/shard_map/ppermute | solution.py:284
  4.7 3.2 %collective-permute-done = bf16[1,64,1024]{2,1,0:T(8,128)(2,1)} collective-permute-done((bf16[1,64,1024]{2,1,0:T(8,128)(2,1)}, bf16[1,64,1024]{2,1,0:T(8,128)(2,1)}, u32[]{:S(2)}, u32[]{:S(2)}) %collective-permute-start) | collective-permute-done | bytes 131104 | tf_op jit(solution)/shard_map/ppermute | solution.py:284
  7.8 189.2 %row.1 = bf16[64,1024]{1,0:T(8,128)(2,1)} custom-call(s32[1]{0:T(128)S(6)} %copy.16.len_ref, bf16[64,1024]{1,0:T(8,128)(2,1)} %bitcast.y_ref, bf16[1024,1024]{1,0:T(8,128)(2,1)} %bitcast.11, bf16[2,1024,3,16,128]{4,3,2,1,0:T(8,128)(2,1)} %e_qkv.1, bf16[2,2048,1024]{2,1,0:T(8,128)(2,1)} %bitcast.7, bf16[2,1024,3072]{2,1,0:T(8,128)(2,1)} %e_1.1, ...), custom_call_target="tpu_custom_call" | custom-call | tf_op jit(solution)/shard_map/row/pallas_call | solution.py:258
  197.1 3.4 %collective-permute-start.1 = (bf16[1,64,1024]{2,1,0:T(8,128)(2,1)}, bf16[1,64,1024]{2,1,0:T(8,128)(2,1)S(1)}, u32[]{:S(2)}, u32[]{:S(2)}) collective-permute-start(bf16[1,64,1024]{2,1,0:T(8,128)(2,1)} %bitcast.12), channel_id=1, source_target_pairs={{0,64},{1,65},{2,66},{3,67},{4,68},{5,69},{6,70},{7,71},{8,72},{9,... | collective-permute-start | bytes 393224 | tf_op jit(solution)/shard_map/ppermute | solution.py:285
  200.5 3.2 %collective-permute-done.1 = bf16[1,64,1024]{2,1,0:T(8,128)(2,1)S(1)} collective-permute-done((bf16[1,64,1024]{2,1,0:T(8,128)(2,1)}, bf16[1,64,1024]{2,1,0:T(8,128)(2,1)S(1)}, u32[]{:S(2)}, u32[]{:S(2)}) %collective-permute-start.1) | collective-permute-done | bytes 131104 | tf_op jit(solution)/shard_map/ppermute | solution.py:285
  203.6 0.7 copy.17
Async XLA Ops:
  0.0 7.8 %collective-permute-start = (bf16[1,64,1024]{2,1,0:T(8,128)(2,1)}, bf16[1,64,1024]{2,1,0:T(8,128)(2,1)}, u32[]{:S(2)}, u32[]{:S(2)}) collective-permute-start(bf16[1,64,1024]{2,1,0:T(8,128)(2,1)} %param.16), channel_id=1, source_target_pairs={{0,64},{1,65},{2,66},{3,67},{4,68},{5,69},{6,70},{7,71},{8,72},{9,... | collective-permute-start | bytes 393224 | tf_op jit(solution)/shard_map/ppermute | solution.py:284
  197.1 6.6 %collective-permute-start.1 = (bf16[1,64,1024]{2,1,0:T(8,128)(2,1)}, bf16[1,64,1024]{2,1,0:T(8,128)(2,1)S(1)}, u32[]{:S(2)}, u32[]{:S(2)}) collective-permute-start(bf16[1,64,1024]{2,1,0:T(8,128)(2,1)} %bitcast.12), channel_id=1, source_target_pairs={{0,64},{1,65},{2,66},{3,67},{4,68},{5,69},{6,70},{7,71},{8,72},{9,... | collective-permute-start | bytes 393224 | tf_op jit(solution)/shard_map/ppermute | solution.py:285

commit v3 on v2

--- a/solution.py
+++ b/solution.py
@@ -39,8 +39,29 @@
         write(h * 128, matmul(z_ref[...], w).astype(BF16))
 
 
+def project16(z, w_ref, stage, write):
+    def fill(k):
+        c, rows = k % 4, slice(k // 4 * 8, k // 4 * 8 + 8)
+        stage[c] = w_ref[c * 256:(c + 1) * 256, rows, :].astype(F32).reshape(256 * 8, 128)
+
+    fill(0)
+    fill(1)
+    total = {}
+    for k in range(8):
+        if k + 2 < 8:
+            fill(k + 2)
+        c = k % 4
+        for h in range(0, 8, 2):
+            w = jnp.concatenate([stage[c, pl.ds(h + u, 256, stride=8), :].astype(BF16) for u in range(2)], axis=1)
+            part = matmul(z[:, c * 256:(c + 1) * 256], w)
+            total[h] = part if c == 0 else total[h] + part
+        if c == 3:
+            for h in range(0, 8, 2):
+                write(k // 4 * 1024 + h * 128, total[h].astype(BF16))
+
+
 def row_kernel(len_ref, y_ref, x, e_qkv, e_o, e_1, e_2, d_qkv, d_o, c_q, c_kv, c_o, d_1, d_2, o_ref,
-               state, xn, qkv, stage, b_qkv, b_o, b_cq, b_co, b_1, b_2, proj, mix, st, z, sems):
+               state, xn, qkv, stage, b_qkv, b_o, b_cq, b_co, b_1, b_2, pair, proj, mix, st, z, sems):
     n, m = state.shape[0], y_ref.shape[0]
     enc, dec = (e_qkv, e_o, e_1, e_2), (d_qkv, d_o, d_1, d_2)
 
@@ -96,7 +117,7 @@
                 copy(enc, 0, t).wait()
 
             def write(col, value):
-                qkv[j, :, col:col + 256] = value
+                qkv[j * 4 + col // 256] = value
 
             project8(xn, b_qkv.at[t], half, stage, write)
 
@@ -109,33 +130,37 @@
         lax.fori_loop(0, 6, qkv_step, 0)
 
         def attn_step(j, _):
-            half, base = j // 4, lax.rem(j, 4) * 256
-            work = [(h, i) for h in range(2) for i in range(n // TQ)]
+            work = [(h, i) for h in range(4) for i in range(n // TQ)]
+
+            def block(h):
+                return 2 * j + h // 2
 
             def cols(h):
-                return pl.ds(pl.multiple_of(base + h * 128, 128), 128)
+                return slice(h % 2 * 128, (h % 2 + 1) * 128)
 
             def score(item):
                 h, i = item
-                keys = jnp.concatenate([qkv[2 + half, :, cols(h)], bias], axis=1)
-                query = jnp.concatenate([qkv[half, i * TQ:(i + 1) * TQ, cols(h)], one], axis=1)
+                keys = jnp.concatenate([qkv[8 + block(h), :, cols(h)], bias], axis=1)
+                query = jnp.concatenate([qkv[block(h), i * TQ:(i + 1) * TQ, cols(h)], one], axis=1)
                 return lax.dot_general(query, keys, NT, preferred_element_type=F32)
 
             s = score(work[0])
             for k, (h, i) in enumerate(work):
                 ahead = score(work[k + 1]) if k + 1 < len(work) else None
-                qkv[half, i * TQ:(i + 1) * TQ, cols(h)] = matmul(probs(s), qkv[4 + half, :, cols(h)]).astype(BF16)
+                pair[h // 2, i * TQ:(i + 1) * TQ, cols(h)] = matmul(probs(s), qkv[16 + block(h), :, cols(h)]).astype(BF16)
                 s = ahead
+            for b in range(2):
+                qkv[2 * j + b] = pair[b]
             return 0
 
-        lax.fori_loop(0, 8, attn_step, 0)
+        lax.fori_loop(0, 4, attn_step, 0)
 
         for i in range(3, 6):
             copy(enc, 0, i).wait()
 
         def ffn_step(j, _):
             rs = pl.ds(pl.multiple_of(j * RB, RB), RB)
-            mixed = jnp.concatenate([qkv[0, rs, :], qkv[1, rs, :]], axis=1)
+            mixed = jnp.concatenate([qkv[c, rs, :] for c in range(8)], axis=1)
             mid = (state[rs, :].astype(F32) + matmul(mixed, b_o[...])).astype(BF16)
             normed = rms_norm(mid)
             total = mid.astype(F32)
@@ -160,7 +185,7 @@
         kv_copy(j).wait()
 
         def write(col, value):
-            qkv[j, :, col:col + 256] = value
+            qkv[j * 4 + col // 256] = value
 
         project8(xn, b_cq, lax.rem(j, 2), stage, write)
 
@@ -184,25 +209,17 @@
 
         z[...] = rms_norm(st[...])
 
-        def qkv_step(j, _):
-            t, half = j // 2, lax.rem(j, 2)
-
-            @pl.when(half == 0)
-            def _():
-                copy(dec, 0, t).wait()
+        def qkv_step(t, _):
+            copy(dec, 0, t).wait()
 
             def write(col, value):
-                proj[t, :, pl.ds(pl.multiple_of(half * 1024 + col, 256), 256)] = value
-
-            project8(z, b_qkv.at[t], half, stage, write)
-
-            @pl.when((half == 1) & (l == 0))
-            def _():
-                copy(dec, 1, t).start()
-
+                proj[t, :, col:col + 256] = value
+
+            project16(z[...], b_qkv.at[t], stage, write)
+            again(lambda: copy(dec, 1, t).start())
             return 0
 
-        lax.fori_loop(0, 6, qkv_step, 0)
+        lax.fori_loop(0, 3, qkv_step, 0)
         heads = [slice(h * 128, (h + 1) * 128) for h in range(16)]
         s = [lax.dot_general(proj[0, :, hs], proj[1, :, hs], NT, preferred_element_type=F32) for hs in heads]
         p = probs(jnp.where(causal, jnp.concatenate(s, axis=0), -1e30))
@@ -214,26 +231,22 @@
         z[...] = rms_norm(st[...])
         cq_copy(0).wait()
 
-        def cq_step(half, _):
-            def write(col, value):
-                proj[0, :, pl.ds(pl.multiple_of(half * 1024 + col, 256), 256)] = value
-
-            project8(z, b_cq, half, stage, write)
-            return 0
-
-        lax.fori_loop(0, 2, cq_step, 0)
+        def write(col, value):
+            proj[0, :, col:col + 256] = value
+
+        project16(z[...], b_cq, stage, write)
         again(lambda: cq_copy(1).start())
         for base in (0, 4):
             s = []
             for g in range(base, base + 4):
                 q = jnp.concatenate([proj[0, :, heads[2 * g + r]] for r in range(2)], axis=0)
                 s.append(lax.dot_general(jnp.concatenate([q, one[:2 * m]], axis=1),
-                                         jnp.concatenate([qkv[2 * l, :, heads[g]], bias], axis=1), NT,
+                                         jnp.concatenate([qkv[8 * l + g // 2, :, heads[g % 2]], bias], axis=1), NT,
                                          preferred_element_type=F32))
             p = [probs(part) for part in s]
             for i in range(4):
                 g = base + i
-                o = matmul(p[i], qkv[2 * l + 1, :, heads[g]]).astype(BF16)
+                o = matmul(p[i], qkv[8 * l + 4 + g // 2, :, heads[g % 2]]).astype(BF16)
                 for r in range(2):
                     mix[:, heads[2 * g + r]] = o[r * m:(r + 1) * m]
         co_copy(0).wait()
@@ -261,11 +274,11 @@
         out_specs=vmem,
         out_shape=jax.ShapeDtypeStruct((m, 1024), BF16),
         scratch_shapes=[
-            pltpu.VMEM((n, 1024), BF16), pltpu.VMEM((n, 1024), BF16), pltpu.VMEM((6, n, 1024), BF16),
+            pltpu.VMEM((n, 1024), BF16), pltpu.VMEM((n, 1024), BF16), pltpu.VMEM((24, n, 256), BF16),
             pltpu.VMEM((4, 2048, 128), F32), pltpu.VMEM((3, 1024, 16, 128), BF16), pltpu.VMEM((2048, 1024), BF16),
             pltpu.VMEM((1024, 16, 128), BF16), pltpu.VMEM((2048, 1024), BF16),
             pltpu.VMEM((1024, 3072), BF16), pltpu.VMEM((3072, 1024), BF16),
-            pltpu.VMEM((3, m, 2048), BF16), pltpu.VMEM((m, 2048), BF16), pltpu.VMEM((m, 1024), BF16),
+            pltpu.VMEM((2, n, 256), BF16), pltpu.VMEM((3, m, 2048), BF16), pltpu.VMEM((m, 2048), BF16), pltpu.VMEM((m, 1024), BF16),
             pltpu.VMEM((m, 1024), BF16), pltpu.SemaphoreType.DMA((11,)),
         ],
         compiler_params=pltpu.CompilerParams(vmem_limit_bytes=67_000_000),

time: 204 us -> 185 us (0.907)
  Pallas kernels: 189 us -> 170 us
    pallas_call x1, Pallas kernels: 189 us -> 170 us  [local(): pl.pallas_call(row_kernel, in_specs=[pl.BlockSpec(memory_space=pltpu.SMEM...]
where the time goes in v3:
time: 185 us
  Pallas kernels  170 us (92%)
  starting transfers between devices  7.4 us (4%)
  waiting for transfers between devices  6.34 us (3%)
    pallas_call x1, Pallas kernels, local(): pl.pallas_call(row_kernel, in_specs=[pl.BlockSpec(memory_space=pltpu.SMEM...  170 us
    ppermute x1, starting transfers between devices, body(): done = local(x_enc, enc_len, lax.ppermute(y, 'stage', swap), *weights)  4.02 us
  transfers between devices with their start and end apart: 2, of which 2 were waited for; matrix products, arithmetic and copies ran while one was open for 0% of the time, Pallas kernels for 0%

profile of v3, /device:TPU:0, one launch (start us, length us, event | category | flops | bytes accessed | tf_op | source)
XLA Modules:
  0.0 184.9 jit_solution(14041504330245889434)
XLA Ops:
  0.0 4.0 %collective-permute-start = (bf16[1,64,1024]{2,1,0:T(8,128)(2,1)}, bf16[1,64,1024]{2,1,0:T(8,128)(2,1)}, u32[]{:S(2)}, u32[]{:S(2)}) collective-permute-start(bf16[1,64,1024]{2,1,0:T(8,128)(2,1)} %param.16), channel_id=1, source_target_pairs={{0,64},{1,65},{2,66},{3,67},{4,68},{5,69},{6,70},{7,71},{8,72},{9,... | collective-permute-start | bytes 393224 | tf_op jit(solution)/shard_map/ppermute | solution.py:297
  4.7 3.2 %collective-permute-done = bf16[1,64,1024]{2,1,0:T(8,128)(2,1)} collective-permute-done((bf16[1,64,1024]{2,1,0:T(8,128)(2,1)}, bf16[1,64,1024]{2,1,0:T(8,128)(2,1)}, u32[]{:S(2)}, u32[]{:S(2)}) %collective-permute-start) | collective-permute-done | bytes 131104 | tf_op jit(solution)/shard_map/ppermute | solution.py:297
  7.8 169.9 %row.1 = bf16[64,1024]{1,0:T(8,128)(2,1)} custom-call(s32[1]{0:T(128)S(6)} %copy.16.len_ref, bf16[64,1024]{1,0:T(8,128)(2,1)} %bitcast.y_ref, bf16[1024,1024]{1,0:T(8,128)(2,1)} %bitcast.11, bf16[2,1024,3,16,128]{4,3,2,1,0:T(8,128)(2,1)} %e_qkv.1, bf16[2,2048,1024]{2,1,0:T(8,128)(2,1)} %bitcast.7, bf16[2,1024,3072]{2,1,0:T(8,128)(2,1)} %e_1.1, ...), custom_call_target="tpu_custom_call" | custom-call | tf_op jit(solution)/shard_map/row/pallas_call | solution.py:271
  177.7 3.4 %collective-permute-start.1 = (bf16[1,64,1024]{2,1,0:T(8,128)(2,1)}, bf16[1,64,1024]{2,1,0:T(8,128)(2,1)S(1)}, u32[]{:S(2)}, u32[]{:S(2)}) collective-permute-start(bf16[1,64,1024]{2,1,0:T(8,128)(2,1)} %bitcast.12), channel_id=1, source_target_pairs={{0,64},{1,65},{2,66},{3,67},{4,68},{5,69},{6,70},{7,71},{8,72},{9,... | collective-permute-start | bytes 393224 | tf_op jit(solution)/shard_map/ppermute | solution.py:298
  181.1 3.2 %collective-permute-done.1 = bf16[1,64,1024]{2,1,0:T(8,128)(2,1)S(1)} collective-permute-done((bf16[1,64,1024]{2,1,0:T(8,128)(2,1)}, bf16[1,64,1024]{2,1,0:T(8,128)(2,1)S(1)}, u32[]{:S(2)}, u32[]{:S(2)}) %collective-permute-start.1) | collective-permute-done | bytes 131104 | tf_op jit(solution)/shard_map/ppermute | solution.py:298
  184.3 0.7 copy.17
Async XLA Ops:
  0.0 7.8 %collective-permute-start = (bf16[1,64,1024]{2,1,0:T(8,128)(2,1)}, bf16[1,64,1024]{2,1,0:T(8,128)(2,1)}, u32[]{:S(2)}, u32[]{:S(2)}) collective-permute-start(bf16[1,64,1024]{2,1,0:T(8,128)(2,1)} %param.16), channel_id=1, source_target_pairs={{0,64},{1,65},{2,66},{3,67},{4,68},{5,69},{6,70},{7,71},{8,72},{9,... | collective-permute-start | bytes 393224 | tf_op jit(solution)/shard_map/ppermute | solution.py:297
  177.7 6.6 %collective-permute-start.1 = (bf16[1,64,1024]{2,1,0:T(8,128)(2,1)}, bf16[1,64,1024]{2,1,0:T(8,128)(2,1)S(1)}, u32[]{:S(2)}, u32[]{:S(2)}) collective-permute-start(bf16[1,64,1024]{2,1,0:T(8,128)(2,1)} %bitcast.12), channel_id=1, source_target_pairs={{0,64},{1,65},{2,66},{3,67},{4,68},{5,69},{6,70},{7,71},{8,72},{9,... | collective-permute-start | bytes 393224 | tf_op jit(solution)/shard_map/ppermute | solution.py:298
